TPU v7x, 32 devices: a whole 2x2x4 slice. The times are simulated.
32 devices in a mesh: batch: 8 (over y, x, core), tensor: 4 (over z).
Axes of the slice: x: 2, y: 2, z: 4, core: 2. Of those that a mesh axis runs over, the one named last changes fastest.
Arguments:
- hidden_in: bfloat16 [32, 512, 768], P(('batch', 'tensor')), may hold values from -6 to 6
- segment_ids: int32 [32, 512], P('batch'), may hold values from 0 to 7, never falling along the last dimension, each value on 1 to 128 neighbouring positions
- query_weight: bfloat16 [768, 768], P(None, 'tensor'), may hold values from -0.21875 to 0.21875
- query_bias: float32 [768], P('tensor'), may hold values from -3 to 3
- key_weight: bfloat16 [768, 768], P(None, 'tensor'), may hold values from -0.21875 to 0.21875
- value_weight: bfloat16 [768, 768], P(None, 'tensor'), may hold values from -0.21875 to 0.21875
- value_bias: float32 [768], P('tensor'), may hold values from -3 to 3
- out_weight: bfloat16 [768, 768], P('tensor'), may hold values from -1.25 to 1.25
- out_bias: float32 [768], replicated, may hold values from -3 to 3
- attn_gain: float32 [768], replicated, may hold values from 0.5 to 1.5
- attn_shift: float32 [768], replicated, may hold values from -3 to 3
- up_weight: bfloat16 [768, 3072], P(None, 'tensor'), may hold values from -0.21875 to 0.21875
- up_bias: float32 [3072], P('tensor'), may hold values from -3 to 3
- down_weight: bfloat16 [3072, 768], P('tensor'), may hold values from -0.109375 to 0.109375
- down_bias: float32 [768], replicated, may hold values from -3 to 3
- ffn_gain: float32 [768], replicated, may hold values from 0.5 to 1.5
- ffn_shift: float32 [768], replicated, may hold values from -3 to 3
- cotangent: bfloat16 [32, 512, 768], P(('batch', 'tensor')), may hold values from -6 to 6
Outputs:
- layer_out: bfloat16 [32, 512, 768], P(('batch', 'tensor'))
- pooled: float32 [32, 8, 768], P(('batch', 'tensor'))
- grad_input: float32 [32, 512, 768], P(('batch', 'tensor'))
- grad_query_weight: float32 [768, 768], P(None, 'tensor')
- grad_query_bias: float32 [768], P('tensor')
- grad_key_weight: float32 [768, 768], P(None, 'tensor')
- grad_value_weight: float32 [768, 768], P(None, 'tensor')
- grad_value_bias: float32 [768], P('tensor')
- grad_out_weight: float32 [768, 768], P('tensor')
- grad_out_bias: float32 [768], P('tensor')
- grad_attn_gain: float32 [768], P('tensor')
- grad_attn_shift: float32 [768], P('tensor')
- grad_up_weight: float32 [768, 3072], P(None, 'tensor')
- grad_up_bias: float32 [3072], P('tensor')
- grad_down_weight: float32 [3072, 768], P('tensor')
- grad_down_bias: float32 [768], P('tensor')
- grad_ffn_gain: float32 [768], P('tensor')
- grad_ffn_shift: float32 [768], P('tensor')
Inputs may be any that keep to these rules, and one draw needn't show every extreme that they name: `segment_ids`: in each row the text numbers never fall, every text 0 to 7 occurs, each has 1 to 128 positions, and some text has exactly 128.
All inputs are finite; a program needn't handle non-finite values.
Results may differ from a plain program's by a relative error of at most 0.015.
Values may be sent and summed in bfloat16 or wider, within the bound.
A program may use at most 128 MiB of HBM per device.

v0:
```python
import math
import jax
import jax.numpy as jnp
from jax import lax
from jax.sharding import PartitionSpec as P

HEAD_DIM = 64
TEXTS = 8


def product(left, right):
    return jnp.dot(left, right, preferred_element_type=jnp.float32)


def through_rows(left, right):
    return lax.dot_general(
        left, right, (((0,), (0,)), ((), ())), preferred_element_type=jnp.float32
    )


def against_cols(left, right):
    return lax.dot_general(
        left, right, (((1,), (1,)), ((), ())), preferred_element_type=jnp.float32
    )


def normalize(resid, gain, shift):
    center = resid - jnp.mean(resid, axis=-1, keepdims=True)
    spread = jnp.mean(center * center, axis=-1, keepdims=True)
    return center * lax.rsqrt(spread + 1e-12) * gain + shift


def gelu_exact(value):
    return jax.nn.gelu(value, approximate=False)


def per_device(
    hidden_in,
    segment_ids,
    query_weight,
    query_bias,
    key_weight,
    value_weight,
    value_bias,
    out_weight,
    out_bias,
    attn_gain,
    attn_shift,
    up_weight,
    up_bias,
    down_weight,
    down_bias,
    ffn_gain,
    ffn_shift,
    cotangent,
):
    local_rows, length, model_width = hidden_in.shape
    inner_width = query_weight.shape[1]
    heads_here = inner_width // HEAD_DIM
    score_scale = 1.0 / math.sqrt(HEAD_DIM)
    gathered = lax.all_gather(hidden_in, "tensor", axis=0, tiled=True)
    all_rows = gathered.shape[0]
    tokens = all_rows * length
    flat_in = gathered.reshape(tokens, model_width)
    query = (product(flat_in, query_weight) + query_bias).astype(jnp.bfloat16)
    keyset = product(flat_in, key_weight).astype(jnp.bfloat16)
    valueset = (product(flat_in, value_weight) + value_bias).astype(jnp.bfloat16)

    def by_heads(tensor):
        return tensor.reshape(all_rows, length, heads_here, HEAD_DIM)

    query_heads, key_heads, value_heads = (by_heads(query), by_heads(keyset), by_heads(valueset))

    def scored(query_row, key_row, segment_row):
        scores = (
            jnp.einsum("qhd,khd->hqk", query_row, key_row, preferred_element_type=jnp.float32)
            * score_scale
        )
        same_text = segment_row[:, None] == segment_row[None, :]
        return jnp.where(same_text[None], scores, -1000000000.0)

    def attend(items):
        query_row, key_row, value_row, segment_row = items
        scores = scored(query_row, key_row, segment_row)
        row_peak = jnp.max(scores, axis=-1, keepdims=True)
        exponent = jnp.exp(scores - row_peak)
        row_total = jnp.sum(exponent, axis=-1, keepdims=True)
        probability = (exponent / row_total).astype(jnp.bfloat16)
        context_row = jnp.einsum(
            "hqk,khd->qhd", probability, value_row, preferred_element_type=jnp.float32
        )
        return (context_row.astype(jnp.bfloat16), row_peak + jnp.log(row_total))

    context, log_totals = lax.map(attend, (query_heads, key_heads, value_heads, segment_ids))
    context = context.reshape(all_rows, length, inner_width)
    input_float = hidden_in.astype(jnp.float32)
    partial_out = product(context.reshape(tokens, inner_width), out_weight).reshape(
        all_rows, length, model_width
    )
    attn = lax.psum_scatter(partial_out, "tensor", scatter_dimension=0, tiled=True)
    hidden1, norm1_pull = jax.vjp(normalize, attn + out_bias + input_float, attn_gain, attn_shift)
    hidden1_low = hidden1.astype(jnp.bfloat16)
    hidden1_all = lax.all_gather(hidden1_low, "tensor", axis=0, tiled=True).reshape(
        tokens, model_width
    )
    preact = product(hidden1_all, up_weight) + up_bias
    activated, gelu_pull = jax.vjp(gelu_exact, preact)
    activated_low = activated.astype(jnp.bfloat16)
    partial_ffn = product(activated_low, down_weight).reshape(all_rows, length, model_width)
    ffn = lax.psum_scatter(partial_ffn, "tensor", scatter_dimension=0, tiled=True)
    final, norm2_pull = jax.vjp(normalize, ffn + down_bias + hidden1, ffn_gain, ffn_shift)
    first_row = lax.axis_index("tensor") * local_rows
    segment_here = lax.dynamic_slice_in_dim(segment_ids, first_row, local_rows, 0)
    labels = jnp.arange(TEXTS, dtype=jnp.int32)
    member = (segment_here[:, None, :] == labels[None, :, None]).astype(jnp.float32)
    counts = jnp.sum(member, axis=-1)
    pooled = (
        jnp.einsum("rts,rsd->rtd", member, final, precision=lax.Precision.HIGHEST)
        / counts[:, :, None]
    )
    dresid2, ffn_gain_part, ffn_shift_part = norm2_pull(cotangent.astype(jnp.float32))
    down_bias_part = jnp.sum(dresid2, axis=(0, 1))
    dffn_low = dresid2.astype(jnp.bfloat16)
    dffn_all = lax.all_gather(dffn_low, "tensor", axis=0, tiled=True).reshape(tokens, model_width)
    grad_down = through_rows(activated_low, dffn_all)
    dactivated = against_cols(dffn_all, down_weight)
    dpreact = gelu_pull(dactivated)[0].astype(jnp.bfloat16)
    grad_up_bias = jnp.sum(dpreact.astype(jnp.float32), axis=0)
    grad_up = through_rows(hidden1_all, dpreact)
    dhidden_part = against_cols(dpreact, up_weight).reshape(all_rows, length, model_width)
    dhidden1 = lax.psum_scatter(dhidden_part, "tensor", scatter_dimension=0, tiled=True) + dresid2
    dresid1, attn_gain_part, attn_shift_part = norm1_pull(dhidden1)
    out_bias_part = jnp.sum(dresid1, axis=(0, 1))
    dattn_low = dresid1.astype(jnp.bfloat16)
    dattn_all = lax.all_gather(dattn_low, "tensor", axis=0, tiled=True).reshape(tokens, model_width)
    grad_out = through_rows(context.reshape(tokens, inner_width), dattn_all)
    dcontext = against_cols(dattn_all, out_weight).astype(jnp.bfloat16)
    dcontext_heads = by_heads(dcontext)

    def attend_back(items):
        query_row, key_row, value_row, segment_row, log_row, dctx_row = items
        scores = scored(query_row, key_row, segment_row)
        probability = jnp.exp(scores - log_row)
        dvalue_row = jnp.einsum(
            "hqk,qhd->khd",
            probability.astype(jnp.bfloat16),
            dctx_row,
            preferred_element_type=jnp.float32,
        ).astype(jnp.bfloat16)
        dprobs = jnp.einsum("qhd,khd->hqk", dctx_row, value_row, preferred_element_type=jnp.float32)
        dscores = (
            probability * (dprobs - jnp.sum(dprobs * probability, axis=-1, keepdims=True))
        ).astype(jnp.bfloat16)
        dquery_row = (
            jnp.einsum("hqk,khd->qhd", dscores, key_row, preferred_element_type=jnp.float32)
            * score_scale
        ).astype(jnp.bfloat16)
        dkey_row = (
            jnp.einsum("hqk,qhd->khd", dscores, query_row, preferred_element_type=jnp.float32)
            * score_scale
        ).astype(jnp.bfloat16)
        return (dquery_row, dkey_row, dvalue_row)

    dquery, dkey, dvalue = lax.map(
        attend_back, (query_heads, key_heads, value_heads, segment_ids, log_totals, dcontext_heads)
    )
    dquery = dquery.reshape(tokens, inner_width)
    dkey = dkey.reshape(tokens, inner_width)
    dvalue = dvalue.reshape(tokens, inner_width)
    grad_query = through_rows(flat_in, dquery)
    grad_query_bias = jnp.sum(dquery.astype(jnp.float32), axis=0)
    grad_key = through_rows(flat_in, dkey)
    grad_value = through_rows(flat_in, dvalue)
    grad_value_bias = jnp.sum(dvalue.astype(jnp.float32), axis=0)
    dinput_part = (
        against_cols(dquery, query_weight)
        + against_cols(dkey, key_weight)
        + against_cols(dvalue, value_weight)
    ).reshape(all_rows, length, model_width)
    vector_terms = jnp.stack(
        [
            out_bias_part,
            attn_gain_part,
            attn_shift_part,
            down_bias_part,
            ffn_gain_part,
            ffn_shift_part,
        ]
    )
    dinput, vector_sums = (
        lax.psum_scatter(
            dinput_part.astype(jnp.bfloat16), "tensor", scatter_dimension=0, tiled=True
        ).astype(jnp.float32),
        lax.psum_scatter(
            vector_terms.astype(jnp.bfloat16), "tensor", scatter_dimension=1, tiled=True
        ).astype(jnp.float32),
    )
    totals = lax.psum(
        (
            grad_query,
            grad_query_bias,
            grad_key,
            grad_value,
            grad_value_bias,
            grad_out,
            grad_up,
            grad_up_bias,
            grad_down,
            vector_sums,
        ),
        "batch",
    )
    vectors = totals[9]
    return (
        final.astype(jnp.bfloat16),
        pooled,
        dinput + dresid1,
        totals[0],
        totals[1],
        totals[2],
        totals[3],
        totals[4],
        totals[5],
        vectors[0],
        vectors[1],
        vectors[2],
        totals[6],
        totals[7],
        totals[8],
        vectors[3],
        vectors[4],
        vectors[5],
    )


def solution(mesh):
    in_specs = (
        P(("batch", "tensor"), None, None),
        P("batch", None),
        P(None, "tensor"),
        P("tensor"),
        P(None, "tensor"),
        P(None, "tensor"),
        P("tensor"),
        P("tensor", None),
        P(),
        P(),
        P(),
        P(None, "tensor"),
        P("tensor"),
        P("tensor", None),
        P(),
        P(),
        P(),
        P(("batch", "tensor"), None, None),
    )
    out_specs = (
        P(("batch", "tensor"), None, None),
        P(("batch", "tensor"), None, None),
        P(("batch", "tensor"), None, None),
        P(None, "tensor"),
        P("tensor"),
        P(None, "tensor"),
        P(None, "tensor"),
        P("tensor"),
        P("tensor", None),
        P("tensor"),
        P("tensor"),
        P("tensor"),
        P(None, "tensor"),
        P("tensor"),
        P("tensor", None),
        P("tensor"),
        P("tensor"),
        P("tensor"),
    )
    return jax.shard_map(
        per_device, mesh=mesh, in_specs=in_specs, out_specs=out_specs, check_vma=False
    )
```

profile of v0, /device:TPU:0, one launch (start us, length us, event | category | flops | bytes accessed | tf_op | source)
XLA Modules:
  0.0 927.1 jit_solution(11372551995541683853)
XLA Ops:
  8.0 67.8 %all-gather.5.cloned.1.call-done = bf16[4,512,768]{2,1,0:T(8,128)(2,1)} async-done(((bf16[1,512,768]{2,1,0:T(8,128)(2,1)}), bf16[4,512,768]{2,1,0:T(8,128)(2,1)}) %all-gather.5.cloned.1.call-update) | async-done | bytes 3145744 | tf_op jit(solution)/shard_map/all_gather | solution.py:61
  75.8 3.2 fusion.60
  80.6 3.1 fusion.61
  84.6 3.1 convolution_convert_fusion.1
  88.5 17.4 %while.26 = (s32[]{:T(128)}, bf16[4,512,3,64]{1,3,2,0:T(8,128)(2,1)S(1)}, f32[4,3,512,1]{2,1,3,0:T(4,128)}, bf16[4,512,3,64]{1,3,2,0:T(8,128)(2,1)}, s32[4,512]{...) while((s32[]{:T(128)}, ...), condition=%wide.region_3.4_spmd, body=%wide.region_0.3_spmd.sunk | while | flops 211122688 | bytes 11336281 | solution.py:94
  90.8 2.0 fusion.154
  95.2 2.0 fusion.154
  99.5 2.0 fusion.154
  105.9 4.9 fusion.81
  110.9 109.5 %reduce-scatter.8.cloned.1.call-done = f32[1,512,768]{2,1,0:T(8,128)} async-done(((f32[4,512,768]{2,1,0:T(8,128)}), f32[1,512,768]{2,1,0:T(8,128)}) %reduce-scatter.8.cloned.1.call-update) | async-done | bytes 1572880 | tf_op jit(solution)/shard_map/reduce_scatter | solution.py:100
  226.1 63.7 %all-gather.7.cloned.1.call-done = bf16[4,512,768]{2,1,0:T(8,128)(2,1)} async-done(((bf16[1,512,768]{2,1,0:T(8,128)(2,1)}), bf16[4,512,768]{2,1,0:T(8,128)(2,1)}) %all-gather.7.cloned.1.call-update) | async-done | bytes 3145744 | tf_op jit(solution)/shard_map/all_gather | solution.py:103
  289.8 18.4 %multiply_convert_fusion.1 = (bf16[2048,768]{1,0:T(8,128)(2,1)S(1)}, f32[2048,768]{1,0:T(8,128)}, f32[2048,768]{1,0:T(8,128)}) fusion(f32[768]{0:T(1024)} %param.34, bf16[2048,768]{1,0:T(8,128)(2,1)} %bitcast.240, bf16[768,768]{1,0:T(8,128)(2,1)S(1)} %copy-done), kind=kOutput, calls=%fused_computation.67 | convolution fusion | flops 2519728128 | bytes 20057088 | tf_op jit(solution)/shard_map/dot_general | solution.py:12
  308.3 4.5 fusion.92
  312.8 109.5 %reduce-scatter.10.cloned.1.call-done = f32[1,512,768]{2,1,0:T(8,128)} async-done(((f32[4,512,768]{2,1,0:T(8,128)}), f32[1,512,768]{2,1,0:T(8,128)}) %reduce-scatter.10.cloned.1.call-update) | async-done | bytes 1572880 | tf_op jit(solution)/shard_map/reduce_scatter | solution.py:110
  422.4 2.1 fusion.88
  431.1 63.5 %all-gather.9.cloned.1.call-done = bf16[4,512,768]{2,1,0:T(8,128)(2,1)} async-done(((bf16[1,512,768]{2,1,0:T(8,128)(2,1)}), bf16[4,512,768]{2,1,0:T(8,128)(2,1)}) %all-gather.9.cloned.1.call-update) | async-done | bytes 3145744 | tf_op jit(solution)/shard_map/all_gather | solution.py:124
  494.7 11.0 %convert_reduce_fusion = (f32[768]{0:T(1024)}, bf16[2048,768]{1,0:T(8,128)(2,1)S(1)}) fusion(f32[2048,768]{1,0:T(8,128)} %get-tuple-element.242, f32[2048,768]{1,0:T(8,128)} %get-tuple-element.260, f32[768]{0:T(1024)} %param.34, bf16[2048,768]{1,0:T(8,128)(2,1)} %bitcast.242, bf16[768,768]{1,0:T(8,128)(2,1)} %param.35), kind=kOutput, calls=%fused_computation.64 | convolution fusion | flops 2442657024 | bytes 20060160 | tf_op jit(solution)/shard_map/dot_general | solution.py:22
  505.7 4.5 fusion.93
  510.3 109.5 %reduce-scatter.12.cloned.1.call-done = f32[1,512,768]{2,1,0:T(8,128)} async-done(((f32[4,512,768]{2,1,0:T(8,128)}), f32[1,512,768]{2,1,0:T(8,128)}) %reduce-scatter.12.cloned.1.call-update) | async-done | bytes 1572880 | tf_op jit(solution)/shard_map/reduce_scatter | solution.py:131
  619.8 2.7 multiply_reduce_fusion.1
  626.9 62.7 %all-gather.11.cloned.1.call-done = bf16[4,512,768]{2,1,0:T(8,128)(2,1)} async-done(((bf16[1,512,768]{2,1,0:T(8,128)(2,1)}), bf16[4,512,768]{2,1,0:T(8,128)(2,1)}) %all-gather.11.cloned.1.call-update) | async-done | bytes 3145744 | tf_op jit(solution)/shard_map/all_gather | solution.py:135
  689.6 3.1 convolution_convert_fusion
  695.4 29.0 %while.27 = (s32[]{:T(128)}, bf16[4,512,3,64]{1,3,2,0:T(8,128)(2,1)S(1)}, bf16[4,512,3,64]{1,3,2,0:T(8,128)(2,1)}, bf16[4,512,3,64]{1,3,2,0:T(8,128)(2,1)}, bf16...) while((s32[]{:T(128)}, ...), condition=%wide.region_18.19_spmd, body=%wide.region_16.18_spmd.sunk | while | flops 511146496 | bytes 26127476 | solution.py:164
  724.5 2.1 copy.90
  730.6 2.8 add_convert_fusion
  735.8 6.2 fusion.98
  742.0 4.2 fusion.97
  758.7 25.2 %all-reduce = (f32[192]{0:T(256)}, f32[192]{0:T(256)}, f32[6,192]{1,0:T(8,128)S(1)}, f32[768]{0:T(1024)}) all-reduce(f32[192]{0:T(256)S(1)} %reduce_sum.226, f32[192]{0:T(256)S(1)} %reduce_sum.228, bf16[6,192]{1,0:T(8,128)(2,1)S(1)} %copy.97, f32[768]{0:T(1024)S(1)} %copy-done.43), channel_id=1, replica_groups=mesh['batch'=8,'tensor'=4] {'batch'}, use_global_device_ids=true, to_apply=%region_22.23 | all-reduce | flops 2304 | bytes 16128 | tf_op jit(solution)/shard_map/psum | solution.py:198
  784.5 8.1 reduce-scatter.14.cloned.1.call-done
  792.7 3.0 convert_add_fusion
  795.7 114.8 %all-reduce.4.cloned.1.call-done = (f32[768,192]{0,1:T(8,128)}, f32[768,192]{0,1:T(8,128)}, f32[768,192]{0,1:T(8,128)}, f32[192,768]{1,0:T(8,128)}, f32[768,768]{1,0:T(8,128)}, /*index=5*/f32[768,768]{1,0:T(8,128)}) async-done(((f32[768,192]{0,1:T(8,128)}, f32[768,192]{0,1:T(8,128)}, f32[768,192]{0,1:T(8,128)}, f32[192,768]{1,0:T(8,128)}, f32[768,768]{1,0:T(8,128)}, /*index=5*/f32[768,768]{1,0:T(8,128)}), ...) | async-done | bytes 7077904 | tf_op jit(solution)/shard_map/psum | solution.py:198
  910.5 2.1 copy.135
  (247 shorter events, 90.6 us)
Async XLA Ops:
  7.2 282.6 %copy-start = (bf16[768,768]{1,0:T(8,128)(2,1)S(1)}, bf16[768,768]{1,0:T(8,128)(2,1)}, u32[]{:S(2)}) copy-start(bf16[768,768]{1,0:T(8,128)(2,1)} %param.33) | copy-start | bytes 3538948
  7.2 68.6 %all-gather.5.cloned.1.call-start = ((), (), s32[]{:S(2)}) async-start(), calls=%async_computation.5 | async-start | bytes 3932160 | tf_op jit(solution)/shard_map/all_gather | solution.py:61
  7.9 212.5 %reduce-scatter.8.cloned.1.call-start = ((), (), s32[]{:S(2)}) async-start(), calls=%async_computation.6 | async-start | bytes 7864320 | tf_op jit(solution)/shard_map/reduce_scatter | solution.py:100
  105.9 4.9 copy-start.7
  105.9 4.9 copy-start.11
  110.8 109.6 %copy-start.44 = (f32[768]{0:T(1024)S(1)}, f32[768]{0:T(1024)}, u32[]{:S(2)}) copy-start(f32[768]{0:T(1024)} %param.30) | copy-start | bytes 9220
  110.8 113.0 %copy-start.25 = (f32[768]{0:T(1024)S(1)}, f32[768]{0:T(1024)}, u32[]{:S(2)}) copy-start(f32[768]{0:T(1024)} %param.31) | copy-start | bytes 9220
  110.8 179.0 %all-gather.7.cloned.1.call-start = ((), (), s32[]{:S(2)}) async-start(), calls=%async_computation.7 | async-start | bytes 3932160 | tf_op jit(solution)/shard_map/all_gather | solution.py:103
  225.7 196.6 %reduce-scatter.10.cloned.1.call-start = ((), (), s32[]{:S(2)}) async-start(), calls=%async_computation.8 | async-start | bytes 7864320 | tf_op jit(solution)/shard_map/reduce_scatter | solution.py:110
  289.8 18.4 %copy-start.47 = (bf16[768,768]{1,0:T(8,128)(2,1)S(1)}, bf16[768,768]{1,0:T(8,128)(2,1)}, u32[]{:S(2)}) copy-start(bf16[768,768]{1,0:T(8,128)(2,1)} %param.35) | copy-start | bytes 3538948
  308.3 4.5 copy-start.49
  312.8 181.9 %all-gather.9.cloned.1.call-start = ((), (), s32[]{:S(2)}) async-start(), calls=%async_computation.9 | async-start | bytes 3932160 | tf_op jit(solution)/shard_map/all_gather | solution.py:124
  424.4 3.3 copy-start.3
  424.5 3.2 copy-start.29
  424.8 2.9 copy-start.31
  430.6 189.3 %reduce-scatter.12.cloned.1.call-start = ((), (), s32[]{:S(2)}) async-start(), calls=%async_computation.10 | async-start | bytes 7864320 | tf_op jit(solution)/shard_map/reduce_scatter | solution.py:131
  505.7 4.5 copy-start.50
  510.2 109.6 %copy-start.28 = (f32[512]{0:T(512)S(1)}, f32[512]{0:T(512)}, u32[]{:S(2)}) copy-start(f32[512]{0:T(512)} %copy-done.27) | copy-start | bytes 6148
  510.2 109.6 %copy-start.34 = (f32[512]{0:T(512)S(1)}, f32[512]{0:T(512)}, u32[]{:S(2)}) copy-start(f32[512]{0:T(512)} %copy-done.33) | copy-start | bytes 6148
  510.3 112.3 %copy-start.36 = (f32[512]{0:T(512)S(1)}, f32[512]{0:T(512)}, u32[]{:S(2)}) copy-start(f32[512]{0:T(512)} %copy-done.35) | copy-start | bytes 6148
  510.3 179.3 %all-gather.11.cloned.1.call-start = ((), (), s32[]{:S(2)}) async-start(), calls=%async_computation.11 | async-start | bytes 3932160 | tf_op jit(solution)/shard_map/all_gather | solution.py:135
  622.6 3.0 copy-start.13
  623.2 66.3 %copy-start.19 = (bf16[192,768]{1,0:T(8,128)(2,1)S(1)}, bf16[192,768]{1,0:T(8,128)(2,1)}, u32[]{:S(2)}) copy-start(bf16[192,768]{1,0:T(8,128)(2,1)} %param.29) | copy-start | bytes 884740
  625.5 130.8 %reduce-scatter.16.cloned.1.call-start = ((), (), s32[]{:S(2)}) async-start(), calls=%async_computation.13 | async-start | bytes 245760
  626.7 166.0 %reduce-scatter.14.cloned.1.call-start = ((), (), s32[]{:S(2)}) async-start(), calls=%async_computation.12 | async-start | bytes 3932160 | tf_op jit(solution)/shard_map/reduce_scatter | solution.py:191
  733.5 177.0 %all-reduce.4.cloned.1.call-start = ((), (), s32[]{:S(2)}) async-start(), calls=%async_computation.14 | async-start | bytes 14155776 | tf_op jit(solution)/shard_map/psum | solution.py:198
  735.8 6.2 copy-start.45
  735.8 6.2 copy-start.51
  742.0 4.2 copy-start.2
  753.4 5.4 copy-start.43
  910.5 5.9 copy-start.18
  910.5 6.7 copy-start.17
  (30 other events, 51.4 us)
Sparse Core Ops, SparseCore 0:
  9.6 66.1 all-gather.4
  110.9 109.4 reduce-scatter.7
  225.9 63.9 all-gather.6
  312.9 109.4 reduce-scatter.9
  430.7 63.9 all-gather.8
  510.4 109.4 reduce-scatter.11
  625.6 63.9 all-gather.10
  691.8 18.2 reduce-scatter.15
  733.6 59.0 reduce-scatter.13
  797.7 112.7 all-reduce.3
where the time goes:
time: 935 us; the launch traced here: 927 us
  waiting for transfers between devices  710 us (76%)
  matrix products  112 us (12%)
  local copies, waits for them, and re-layouts  32.4 us (3%)
  other arithmetic  30.5 us (3%)
  blocking collectives  25.2 us (3%)
  between operations  15 us (2%)
    psum x1, waiting for transfers between devices, per_device(): lax.psum((grad_query, grad_query_bias, grad_key, grad_value, grad_value_b...  115 us
    reduce_scatter x1, waiting for transfers between devices, per_device(): lax.psum_scatter(partial_ffn, 'tensor', scatter_dimension=0, tiled=True)  110 us
    reduce_scatter x1, waiting for transfers between devices, per_device(): lax.psum_scatter(dhidden_part, 'tensor', scatter_dimension=0, tiled=True)  110 us
    reduce_scatter x1, waiting for transfers between devices, per_device(): lax.psum_scatter(partial_out, 'tensor', scatter_dimension=0, tiled=True)  110 us
    all_gather x1, waiting for transfers between devices, per_device(): gathered = lax.all_gather(hidden_in, 'tensor', axis=0, tiled=True)  67.8 us
    all_gather x1, waiting for transfers between devices, per_device(): lax.all_gather(hidden1_low, 'tensor', axis=0, tiled=True)  63.7 us
    all_gather x1, waiting for transfers between devices, per_device(): lax.all_gather(dffn_low, 'tensor', axis=0, tiled=True)  63.5 us
    all_gather x1, waiting for transfers between devices, per_device(): lax.all_gather(dattn_low, 'tensor', axis=0, tiled=True)  62.7 us
  transfers between devices with their start and end apart: 10, of which 9 were waited for; matrix products, arithmetic and copies ran while one was open for 8% of the time, Pallas kernels for 0%

commit v1 on v0

--- a/solution.py
+++ b/solution.py
@@ -6,6 +6,28 @@
 
 HEAD_DIM = 64
 TEXTS = 8
+
+
+def in_order(pieces, dim):
+    pieces = jnp.moveaxis(pieces, 0, dim)
+    shape = pieces.shape
+    return pieces.reshape(*shape[:dim], shape[dim] * shape[dim + 1], *shape[dim + 2 :])
+
+
+def ring_gather(x, axis, dim):
+    size = lax.axis_size(axis)
+    pairs = [(i, (i + 1) % size) for i in range(size)]
+    back = [(b, a) for a, b in pairs]
+    lower, upper = ([], [])
+    for turn in range(size - 1):
+        if turn % 2 == 0:
+            lower.append(lax.ppermute(lower[-1] if lower else x, axis, pairs))
+        else:
+            upper.append(lax.ppermute(upper[-1] if upper else x, axis, back))
+    blocks = jnp.stack([*lower[::-1], x, *upper])
+    shift = lax.axis_index(axis) - len(lower)
+    blocks = blocks[(jnp.arange(size) - shift) % size]
+    return in_order(blocks, dim)
 
 
 def product(left, right):
@@ -121,7 +143,7 @@
     dresid2, ffn_gain_part, ffn_shift_part = norm2_pull(cotangent.astype(jnp.float32))
     down_bias_part = jnp.sum(dresid2, axis=(0, 1))
     dffn_low = dresid2.astype(jnp.bfloat16)
-    dffn_all = lax.all_gather(dffn_low, "tensor", axis=0, tiled=True).reshape(tokens, model_width)
+    dffn_all = ring_gather(dffn_low, "tensor", 0).reshape(tokens, model_width)
     grad_down = through_rows(activated_low, dffn_all)
     dactivated = against_cols(dffn_all, down_weight)
     dpreact = gelu_pull(dactivated)[0].astype(jnp.bfloat16)

time: 935 us -> 934 us (level)
  waiting for transfers between devices: 710 us -> 683 us
  starting transfers between devices: 1.61 us -> 19.9 us
    all_gather x1 -> x0, waiting for transfers between devices: 63.5 us -> none  [per_device(): lax.all_gather(dffn_low, 'tensor', axis=0, tiled=True)]
    ppermute x0 -> x3, waiting for transfers between devices: none -> 35.6 us  [the longest x2 35.1 us: ring_gather(): lower.append(lax.ppermute(lower[-1] if lower else x, axis, pairs))]
    ppermute x0 -> x3, starting transfers between devices: none -> 18.8 us  [the longest x2 16.5 us: ring_gather(): lower.append(lax.ppermute(lower[-1] if lower else x, axis, pairs))]
  transfers between devices with their start and end apart: 10 -> 12, of which waited for: 9 -> 11; matrix products, arithmetic and copies ran while one was open for 8% -> 8% of each run, Pallas kernels for 0% -> 0%
where the time goes in v1:
time: 934 us; the launch traced here: 926 us
  waiting for transfers between devices  683 us (73%)
  matrix products  112 us (12%)
  local copies, waits for them, and re-layouts  36.6 us (4%)
  other arithmetic  34.4 us (4%)
  blocking collectives  25.2 us (3%)
  starting transfers between devices  19.9 us (2%)
  between operations  14.7 us (2%)
    psum x1, waiting for transfers between devices, per_device(): lax.psum((grad_query, grad_query_bias, grad_key, grad_value, grad_value_b...  115 us
    reduce_scatter x1, waiting for transfers between devices, per_device(): lax.psum_scatter(dhidden_part, 'tensor', scatter_dimension=0, tiled=True)  110 us
    reduce_scatter x1, waiting for transfers between devices, per_device(): lax.psum_scatter(partial_ffn, 'tensor', scatter_dimension=0, tiled=True)  110 us
    reduce_scatter x1, waiting for transfers between devices, per_device(): lax.psum_scatter(partial_out, 'tensor', scatter_dimension=0, tiled=True)  110 us
    all_gather x1, waiting for transfers between devices, per_device(): gathered = lax.all_gather(hidden_in, 'tensor', axis=0, tiled=True)  67.8 us
    all_gather x1, waiting for transfers between devices, per_device(): lax.all_gather(hidden1_low, 'tensor', axis=0, tiled=True)  63.7 us
    all_gather x1, waiting for transfers between devices, per_device(): lax.all_gather(dattn_low, 'tensor', axis=0, tiled=True)  62.7 us
    dot_general x6, matrix products, product(): return jnp.dot(left, right, preferred_element_type=jnp.float32)  37.1 us
  transfers between devices with their start and end apart: 12, of which 11 were waited for; matrix products, arithmetic and copies ran while one was open for 8% of the time, Pallas kernels for 0%

profile of v1, /device:TPU:0, one launch (start us, length us, event | category | flops | bytes accessed | tf_op | source)
XLA Modules:
  0.0 925.9 jit_solution(2860677074714312913)
XLA Ops:
  8.0 67.8 %all-gather.4.cloned.1.call-done = bf16[4,512,768]{2,1,0:T(8,128)(2,1)} async-done(((bf16[1,512,768]{2,1,0:T(8,128)(2,1)}), bf16[4,512,768]{2,1,0:T(8,128)(2,1)}) %all-gather.4.cloned.1.call-update) | async-done | bytes 3145744 | tf_op jit(solution)/shard_map/all_gather | solution.py:83
  75.8 3.2 fusion.60
  80.6 3.1 fusion.61
  84.4 3.1 convolution_convert_fusion.1
  88.3 17.4 %while.26 = (s32[]{:T(128)}, bf16[4,512,3,64]{1,3,2,0:T(8,128)(2,1)S(1)}, f32[4,3,512,1]{2,1,3,0:T(4,128)}, bf16[4,512,3,64]{1,3,2,0:T(8,128)(2,1)}, s32[4,512]{...) while((s32[]{:T(128)}, ...), condition=%wide.region_3.4_spmd, body=%wide.region_0.3_spmd.sunk | while | flops 211122688 | bytes 11336281 | solution.py:116
  105.7 4.9 fusion.81
  110.7 109.5 %reduce-scatter.8.cloned.1.call-done = f32[1,512,768]{2,1,0:T(8,128)} async-done(((f32[4,512,768]{2,1,0:T(8,128)}), f32[1,512,768]{2,1,0:T(8,128)}) %reduce-scatter.8.cloned.1.call-update) | async-done | bytes 1572880 | tf_op jit(solution)/shard_map/reduce_scatter | solution.py:122
  225.9 63.7 %all-gather.6.cloned.1.call-done = bf16[4,512,768]{2,1,0:T(8,128)(2,1)} async-done(((bf16[1,512,768]{2,1,0:T(8,128)(2,1)}), bf16[4,512,768]{2,1,0:T(8,128)(2,1)}) %all-gather.6.cloned.1.call-update) | async-done | bytes 3145744 | tf_op jit(solution)/shard_map/all_gather | solution.py:125
  289.6 18.4 %multiply_convert_fusion.1 = (bf16[2048,768]{1,0:T(8,128)(2,1)S(1)}, f32[2048,768]{1,0:T(8,128)}, f32[2048,768]{1,0:T(8,128)}) fusion(f32[768]{0:T(1024)} %param.34, bf16[2048,768]{1,0:T(8,128)(2,1)} %bitcast.250, bf16[768,768]{1,0:T(8,128)(2,1)S(1)} %copy-done), kind=kOutput, calls=%fused_computation.68 | convolution fusion | flops 2519728128 | bytes 20057088 | tf_op jit(solution)/shard_map/dot_general | solution.py:34
  308.1 4.5 fusion.94
  312.6 109.5 %reduce-scatter.10.cloned.1.call-done = f32[1,512,768]{2,1,0:T(8,128)} async-done(((f32[4,512,768]{2,1,0:T(8,128)}), f32[1,512,768]{2,1,0:T(8,128)}) %reduce-scatter.10.cloned.1.call-update) | async-done | bytes 1572880 | tf_op jit(solution)/shard_map/reduce_scatter | solution.py:132
  422.1 2.1 fusion.90
  431.8 2.4 collective-permute-start.2
  434.1 18.7 %collective-permute-done = bf16[1,512,768]{2,1,0:T(8,128)(2,1)} collective-permute-done((bf16[1,512,768]{2,1,0:T(8,128)(2,1)}, bf16[1,512,768]{2,1,0:T(8,128)(2,1)}, u32[]{:S(2)}, u32[]{:S(2)}) %collective-permute-start) | collective-permute-done | bytes 786464 | tf_op jit(solution)/shard_map/ppermute | solution.py:24
  452.9 15.0 %collective-permute-start.1 = (bf16[1,512,768]{2,1,0:T(8,128)(2,1)}, bf16[1,512,768]{2,1,0:T(8,128)(2,1)}, u32[]{:S(2)}, u32[]{:S(2)}) collective-permute-start(bf16[1,512,768]{2,1,0:T(8,128)(2,1)} %collective-permute-done), channel_id=1, source_target_pairs={{0,1},{1,2},{2,3},{3,0},{4,5},{5,6},{6,7},{7,4},{8,9},{9,10},{10,1... | collective-permute-start | bytes 2359304 | tf_op jit(solution)/shard_map/ppermute | solution.py:24
  469.1 16.3 %collective-permute-done.1 = bf16[1,512,768]{2,1,0:T(8,128)(2,1)} collective-permute-done((bf16[1,512,768]{2,1,0:T(8,128)(2,1)}, bf16[1,512,768]{2,1,0:T(8,128)(2,1)}, u32[]{:S(2)}, u32[]{:S(2)}) %collective-permute-start.1) | collective-permute-done | bytes 786464 | tf_op jit(solution)/shard_map/ppermute | solution.py:24
  485.4 3.3 maximum_bitcast_fusion
  488.7 4.4 gather_fusion
  493.1 11.0 %convert_reduce_fusion = (f32[768]{0:T(1024)}, bf16[2048,768]{1,0:T(8,128)(2,1)S(1)}) fusion(f32[2048,768]{1,0:T(8,128)} %get-tuple-element.242, f32[2048,768]{1,0:T(8,128)} %get-tuple-element.260, f32[768]{0:T(1024)} %param.34, bf16[2048,768]{1,0:T(8,128)(2,1)} %bitcast.229, bf16[768,768]{1,0:T(8,128)(2,1)} %param.35), kind=kOutput, calls=%fused_computation.65 | convolution fusion | flops 2442657024 | bytes 20060160 | tf_op jit(solution)/shard_map/dot_general | solution.py:44
  504.1 4.5 fusion.95
  508.7 110.0 %reduce-scatter.12.cloned.1.call-done = f32[1,512,768]{2,1,0:T(8,128)} async-done(((f32[4,512,768]{2,1,0:T(8,128)}), f32[1,512,768]{2,1,0:T(8,128)}) %reduce-scatter.12.cloned.1.call-update) | async-done | bytes 1572880 | tf_op jit(solution)/shard_map/reduce_scatter | solution.py:153
  618.7 2.7 multiply_reduce_fusion.1
  625.8 62.7 %all-gather.8.cloned.1.call-done = bf16[4,512,768]{2,1,0:T(8,128)(2,1)} async-done(((bf16[1,512,768]{2,1,0:T(8,128)(2,1)}), bf16[4,512,768]{2,1,0:T(8,128)(2,1)}) %all-gather.8.cloned.1.call-update) | async-done | bytes 3145744 | tf_op jit(solution)/shard_map/all_gather | solution.py:157
  688.5 3.0 convolution_convert_fusion
  694.3 29.1 %while.27 = (s32[]{:T(128)}, bf16[4,512,3,64]{1,3,2,0:T(8,128)(2,1)S(1)}, bf16[4,512,3,64]{1,3,2,0:T(8,128)(2,1)}, bf16[4,512,3,64]{1,3,2,0:T(8,128)(2,1)}, bf16...) while((s32[]{:T(128)}, ...), condition=%wide.region_18.19_spmd, body=%wide.region_16.18_spmd.sunk | while | flops 511146496 | bytes 26127476 | solution.py:186
  729.6 2.8 add_convert_fusion
  734.8 6.2 fusion.100
  741.0 4.2 fusion.99
  757.7 25.2 %all-reduce = (f32[192]{0:T(256)}, f32[192]{0:T(256)}, f32[6,192]{1,0:T(8,128)S(1)}, f32[768]{0:T(1024)}) all-reduce(f32[192]{0:T(256)S(1)} %reduce_sum.226, f32[192]{0:T(256)S(1)} %reduce_sum.228, bf16[6,192]{1,0:T(8,128)(2,1)S(1)} %copy.97, f32[768]{0:T(1024)S(1)} %copy-done.43), channel_id=1, replica_groups=mesh['batch'=8,'tensor'=4] {'batch'}, use_global_device_ids=true, to_apply=%region_22.23 | all-reduce | flops 2304 | bytes 16128 | tf_op jit(solution)/shard_map/psum | solution.py:220
  783.5 8.2 reduce-scatter.14.cloned.1.call-done
  791.6 3.0 convert_add_fusion
  794.6 114.9 %all-reduce.4.cloned.1.call-done = (f32[768,192]{0,1:T(8,128)}, f32[768,192]{0,1:T(8,128)}, f32[768,192]{0,1:T(8,128)}, f32[192,768]{1,0:T(8,128)}, f32[768,768]{1,0:T(8,128)}, /*index=5*/f32[768,768]{1,0:T(8,128)}) async-done(((f32[768,192]{0,1:T(8,128)}, f32[768,192]{0,1:T(8,128)}, f32[768,192]{0,1:T(8,128)}, f32[192,768]{1,0:T(8,128)}, f32[768,768]{1,0:T(8,128)}, /*index=5*/f32[768,768]{1,0:T(8,128)}), ...) | async-done | bytes 7077904 | tf_op jit(solution)/shard_map/psum | solution.py:220
  (252 shorter events, 102.6 us)
Async XLA Ops:
  7.2 282.4 %copy-start = (bf16[768,768]{1,0:T(8,128)(2,1)S(1)}, bf16[768,768]{1,0:T(8,128)(2,1)}, u32[]{:S(2)}) copy-start(bf16[768,768]{1,0:T(8,128)(2,1)} %param.33) | copy-start | bytes 3538948
  7.2 68.6 %all-gather.4.cloned.1.call-start = ((), (), s32[]{:S(2)}) async-start(), calls=%async_computation.5 | async-start | bytes 3932160 | tf_op jit(solution)/shard_map/all_gather | solution.py:83
  7.9 212.3 %reduce-scatter.8.cloned.1.call-start = ((), (), s32[]{:S(2)}) async-start(), calls=%async_computation.6 | async-start | bytes 7864320 | tf_op jit(solution)/shard_map/reduce_scatter | solution.py:122
  105.7 4.9 copy-start.7
  105.7 4.9 copy-start.11
  110.6 109.6 %copy-start.44 = (f32[768]{0:T(1024)S(1)}, f32[768]{0:T(1024)}, u32[]{:S(2)}) copy-start(f32[768]{0:T(1024)} %param.30) | copy-start | bytes 9220
  110.6 113.0 %copy-start.25 = (f32[768]{0:T(1024)S(1)}, f32[768]{0:T(1024)}, u32[]{:S(2)}) copy-start(f32[768]{0:T(1024)} %param.31) | copy-start | bytes 9220
  110.6 179.0 %all-gather.6.cloned.1.call-start = ((), (), s32[]{:S(2)}) async-start(), calls=%async_computation.7 | async-start | bytes 3932160 | tf_op jit(solution)/shard_map/all_gather | solution.py:125
  225.5 196.6 %reduce-scatter.10.cloned.1.call-start = ((), (), s32[]{:S(2)}) async-start(), calls=%async_computation.8 | async-start | bytes 7864320 | tf_op jit(solution)/shard_map/reduce_scatter | solution.py:132
  289.6 18.4 %copy-start.46 = (bf16[768,768]{1,0:T(8,128)(2,1)S(1)}, bf16[768,768]{1,0:T(8,128)(2,1)}, u32[]{:S(2)}) copy-start(bf16[768,768]{1,0:T(8,128)(2,1)} %param.35) | copy-start | bytes 3538948
  308.1 4.5 copy-start.48
  312.5 306.2 %reduce-scatter.12.cloned.1.call-start = ((), (), s32[]{:S(2)}) async-start(), calls=%async_computation.9 | async-start | bytes 7864320 | tf_op jit(solution)/shard_map/reduce_scatter | solution.py:153
  424.2 3.3 copy-start.3
  424.2 3.2 copy-start.29
  430.3 22.6 %collective-permute-start = (bf16[1,512,768]{2,1,0:T(8,128)(2,1)}, bf16[1,512,768]{2,1,0:T(8,128)(2,1)}, u32[]{:S(2)}, u32[]{:S(2)}) collective-permute-start(bf16[1,512,768]{2,1,0:T(8,128)(2,1)} %get-tuple-element.251), channel_id=1, source_target_pairs={{0,1},{1,2},{2,3},{3,0},{4,5},{5,6},{6,7},{7,4},{8,9},{9,10},{10,1... | collective-permute-start | bytes 2359304 | tf_op jit(solution)/shard_map/ppermute | solution.py:24
  431.8 37.3 %collective-permute-start.2 = (bf16[1,512,768]{2,1,0:T(8,128)(2,1)}, bf16[1,512,768]{2,1,0:T(8,128)(2,1)}, u32[]{:S(2)}, u32[]{:S(2)}) collective-permute-start(bf16[1,512,768]{2,1,0:T(8,128)(2,1)} %get-tuple-element.251), channel_id=1, source_target_pairs={{1,0},{2,1},{3,2},{0,3},{5,4},{6,5},{7,6},{4,7},{9,8},{10,9},{11,1... | collective-permute-start | bytes 2359304 | tf_op jit(solution)/shard_map/ppermute | solution.py:26
  452.9 32.5 %collective-permute-start.1 = (bf16[1,512,768]{2,1,0:T(8,128)(2,1)}, bf16[1,512,768]{2,1,0:T(8,128)(2,1)}, u32[]{:S(2)}, u32[]{:S(2)}) collective-permute-start(bf16[1,512,768]{2,1,0:T(8,128)(2,1)} %collective-permute-done), channel_id=1, source_target_pairs={{0,1},{1,2},{2,3},{3,0},{4,5},{5,6},{6,7},{7,4},{8,9},{9,10},{10,1... | collective-permute-start | bytes 2359304 | tf_op jit(solution)/shard_map/ppermute | solution.py:24
  504.1 4.5 copy-start.49
  508.6 110.1 %copy-start.28 = (f32[512]{0:T(512)S(1)}, f32[512]{0:T(512)}, u32[]{:S(2)}) copy-start(f32[512]{0:T(512)} %copy-done.27) | copy-start | bytes 6148
  508.6 110.1 %copy-start.34 = (f32[512]{0:T(512)S(1)}, f32[512]{0:T(512)}, u32[]{:S(2)}) copy-start(f32[512]{0:T(512)} %copy-done.33) | copy-start | bytes 6148
  508.7 112.8 %copy-start.36 = (f32[512]{0:T(512)S(1)}, f32[512]{0:T(512)}, u32[]{:S(2)}) copy-start(f32[512]{0:T(512)} %copy-done.35) | copy-start | bytes 6148
  508.7 179.8 %all-gather.8.cloned.1.call-start = ((), (), s32[]{:S(2)}) async-start(), calls=%async_computation.10 | async-start | bytes 3932160 | tf_op jit(solution)/shard_map/all_gather | solution.py:157
  622.1 66.4 %copy-start.20 = (bf16[192,768]{1,0:T(8,128)(2,1)S(1)}, bf16[192,768]{1,0:T(8,128)(2,1)}, u32[]{:S(2)}) copy-start(bf16[192,768]{1,0:T(8,128)(2,1)} %param.29) | copy-start | bytes 884740
  624.4 130.8 %reduce-scatter.16.cloned.1.call-start = ((), (), s32[]{:S(2)}) async-start(), calls=%async_computation.12 | async-start | bytes 245760
  625.6 166.0 %reduce-scatter.14.cloned.1.call-start = ((), (), s32[]{:S(2)}) async-start(), calls=%async_computation.11 | async-start | bytes 3932160 | tf_op jit(solution)/shard_map/reduce_scatter | solution.py:213
  732.4 177.2 %all-reduce.4.cloned.1.call-start = ((), (), s32[]{:S(2)}) async-start(), calls=%async_computation.13 | async-start | bytes 14155776 | tf_op jit(solution)/shard_map/psum | solution.py:220
  734.8 6.2 copy-start.45
  734.8 6.2 copy-start.50
  741.0 4.2 copy-start.2
  752.3 5.4 copy-start.43
  909.6 5.9 copy-start.19
  909.6 6.7 copy-start.18
  (31 other events, 56.3 us)
Sparse Core Ops, SparseCore 0:
  9.6 66.1 all-gather.3
  110.7 109.4 reduce-scatter.7
  225.7 63.9 all-gather.5
  312.7 109.4 reduce-scatter.9
  508.8 109.8 reduce-scatter.11
  624.5 63.9 all-gather.7
  690.7 18.2 reduce-scatter.15
  732.5 59.0 reduce-scatter.13
  796.8 112.6 all-reduce.3
